TPU v7x, 256 devices: a whole 4x4x8 slice. The times are simulated.
256 devices in a mesh: dp: 32 (over z, y_hi, core), tensor: 8 (over x, y_lo).
Axes of the slice: x: 4, y: 4 (y_hi: 2, y_lo: 2; y = y_hi * 2 + y_lo), z: 8, core: 2. Of those that a mesh axis runs over, the one named last changes fastest.
Arguments:
- tokens: bfloat16 [128, 576, 1024], P('dp', 'tensor'), may hold values from -150 to 150
- cotangent: bfloat16 [128, 576, 1024], P('dp', 'tensor'), may hold values from -6 to 6
- dispatch_weight: bfloat16 [1024, 64], replicated, may hold values from -3 to 3
- w_in: bfloat16 [64, 1024, 4096], P('dp', None, 'tensor'), may hold values from -0.1875 to 0.1875
- w_out: bfloat16 [64, 4096, 1024], P('dp', 'tensor'), may hold values from -0.09375 to 0.09375
Outputs:
- grad_tokens: bfloat16 [128, 576, 1024], P('dp', 'tensor')
- grad_router: float32 [1024, 64], replicated
- grad_w_in: bfloat16 [64, 1024, 4096], P('dp', None, 'tensor')
- grad_w_out: bfloat16 [64, 4096, 1024], P('dp', 'tensor')
All inputs are finite; a program needn't handle non-finite values.
Results may differ from a plain program's by a relative error of at most 0.0079.
Values may be sent and summed in bfloat16 or wider, within the bound.
A program may use at most 64 MiB of HBM per device.

v0:
```python
import jax
import jax.numpy as jnp
from jax import lax
from jax.sharding import PartitionSpec as P


def split_up(x, dim, length):
    lengths = x.shape
    blocks = x.reshape(*lengths[:dim], length, lengths[dim] // length, *lengths[dim + 1 :])
    return jnp.moveaxis(blocks, dim, 0)


def summed_on_arrival(x, axis, dim):
    blocks = split_up(x, dim, lax.axis_size(axis))
    arrived = lax.all_to_all(blocks, axis, split_axis=0, concat_axis=0, tiled=True)
    return arrived.sum(axis=0)


def sent_to_all(x, axis):
    length = lax.axis_size(axis)
    return lax.all_to_all(jnp.broadcast_to(x[None], (length, *x.shape)), axis, 0, 0, tiled=True)


def laid_out(blocks, dim):
    lengths = list(blocks.shape[1:])
    lengths[dim] *= blocks.shape[0]
    return jnp.moveaxis(blocks, 0, dim).reshape(lengths)


def gathered_copies(x, axis, dim):
    blocks = sent_to_all(x, axis)
    return laid_out(blocks, dim)


def collected_together(x, axis):
    leaves = jax.tree.leaves(x)
    sequence = sorted(range(len(leaves)), key=lambda k: -leaves[k].size)
    width = (1, *leaves[sequence[0]].shape)[-1]
    lines = [
        jnp.pad(leaves[k].reshape(-1), (0, -leaves[k].size % width)).reshape(-1, width)
        for k in sequence
    ]
    both, at, found = (sent_to_all(jnp.concatenate(lines), axis), 0, {})
    for k, line in zip(sequence, lines):
        piece = both[:, at : at + len(line)].reshape(len(both), -1)
        found[k] = piece[:, : leaves[k].size].reshape(-1, *leaves[k].shape)
        at += len(line)
    numbers = iter(range(len(leaves)))
    return jax.tree.map(lambda _: found[next(numbers)], x)


def combined_pairwise(pieces, combine):
    while len(jax.tree.leaves(pieces)[0]) > 1:
        pieces = jax.vmap(combine)(
            *(jax.tree.map(lambda part: part[side::2], pieces) for side in (0, 1))
        )
    return jax.tree.map(lambda part: part[0], pieces)


def merged(x, axis, combine):
    pieces = collected_together(x, axis)
    return combined_pairwise(pieces, combine)


def over_copies(x, axis):
    return sent_to_all(x, axis).sum(axis=0)


def to_experts(partial_rows):
    shared_part = summed_on_arrival(partial_rows, "tensor", 2).astype(jnp.bfloat16)
    arrived = lax.all_to_all(shared_part, "dp", split_axis=1, concat_axis=0, tiled=True)
    result = gathered_copies(arrived, "tensor", 2)
    return result


def to_images(partial_rows):
    shared_part = summed_on_arrival(partial_rows, "tensor", 2).astype(jnp.bfloat16)
    arrived = lax.all_to_all(shared_part, "dp", split_axis=0, concat_axis=1, tiled=True)
    result = gathered_copies(arrived, "tensor", 2)
    return result


def join_stats(former, latter):
    biggest = jnp.maximum(former[0], latter[0])
    return (
        biggest,
        former[1] * jnp.exp(former[0] - biggest) + latter[1] * jnp.exp(latter[0] - biggest),
    )


def dispatch_softmax(logits):
    local_max = jnp.max(logits, axis=1)
    local_total = jnp.sum(jnp.exp(logits - local_max[:, None, :]), axis=1)
    global_max, totals = merged((local_max, local_total), "tensor", join_stats)
    exponent = jnp.exp(logits - global_max[:, None, :])
    return exponent / totals[:, None, :]


def on_device(tokens, cotangent, dispatch_weight, w_in, w_out):
    wide = jnp.float32
    logits = jnp.einsum("isd,de->ise", tokens, dispatch_weight, preferred_element_type=wide)
    dispatch = dispatch_softmax(logits)
    combine = jax.nn.softmax(logits, axis=2)
    dispatch_low = dispatch.astype(jnp.bfloat16)
    combine_low = combine.astype(jnp.bfloat16)
    slot_inputs = to_experts(
        jnp.einsum("ise,isd->ied", dispatch_low, tokens, preferred_element_type=wide)
    )
    pre_act = jnp.einsum("ied,edf->ief", slot_inputs, w_in, preferred_element_type=wide)
    hidden_act, gelu_back = jax.vjp(jax.nn.gelu, pre_act)
    hidden_low = hidden_act.astype(jnp.bfloat16)
    slot_outputs = to_images(
        jnp.einsum("ief,efd->ied", hidden_low, w_out, preferred_element_type=wide)
    )
    grad_combine = jnp.einsum("isd,ied->ise", cotangent, slot_outputs, preferred_element_type=wide)
    grad_slots_out = to_experts(
        jnp.einsum("ise,isd->ied", combine_low, cotangent, preferred_element_type=wide)
    )
    grad_hidden = jnp.einsum("ied,efd->ief", grad_slots_out, w_out, preferred_element_type=wide)
    grad_pre = gelu_back(grad_hidden)[0].astype(jnp.bfloat16)
    grad_w_out = jnp.einsum(
        "ief,ied->efd", hidden_low, grad_slots_out, preferred_element_type=wide
    ).astype(jnp.bfloat16)
    grad_w_in = jnp.einsum(
        "ied,ief->edf", slot_inputs, grad_pre, preferred_element_type=wide
    ).astype(jnp.bfloat16)
    grad_slots_in = to_images(
        jnp.einsum("ief,edf->ied", grad_pre, w_in, preferred_element_type=wide)
    )
    grad_dispatch = jnp.einsum("isd,ied->ise", tokens, grad_slots_in, preferred_element_type=wide)
    column_dot = over_copies(jnp.sum(grad_dispatch * dispatch, axis=1), "tensor")
    row_dot = jnp.sum(grad_combine * combine, axis=2, keepdims=True)
    grad_logits = (
        combine * (grad_combine - row_dot) + dispatch * (grad_dispatch - column_dot[:, None, :])
    ).astype(jnp.bfloat16)
    token_part = jnp.einsum(
        "ise,ied->isd", dispatch_low, grad_slots_in, preferred_element_type=wide
    )
    router_part = jnp.einsum(
        "ise,de->isd", grad_logits, dispatch_weight, preferred_element_type=wide
    )
    grad_tokens = (token_part + router_part).astype(jnp.bfloat16)
    local_router = jnp.einsum("isd,ise->de", tokens, grad_logits, preferred_element_type=wide)
    grad_router = lax.psum(local_router, ("dp", "tensor"))
    return (grad_tokens, grad_router, grad_w_in, grad_w_out)


def solution(mesh):
    return jax.shard_map(
        on_device,
        mesh=mesh,
        in_specs=(
            P("dp", "tensor", None),
            P("dp", "tensor", None),
            P(),
            P("dp", None, "tensor"),
            P("dp", "tensor", None),
        ),
        out_specs=(P("dp", "tensor", None), P(), P("dp", None, "tensor"), P("dp", "tensor", None)),
        check_vma=False,
    )
```

profile of v0, /device:TPU:2, one launch (start us, length us, event | category | flops | bytes accessed | tf_op | source)
XLA Modules:
  0.0 496.0 jit_solution(7292811887007530040)
XLA Ops:
  9.2 10.4 %all_to_all.110 = f32[8,1,512]{2,1,0:T(1,128)S(1)} all-to-all(f32[8,1,512]{2,1,0:T(1,128)S(1)} %reshape.63), channel_id=1, replica_groups=mesh['dp'=32,'tensor'=8] {'tensor'}, dimensions={0} | all-to-all | bytes 32768 | tf_op jit(solution)/shard_map/all_to_all | solution.py:21
  23.4 5.6 %all-to-all-start.4 = ((f32[8,4,64,128]{3,2,1,0:T(8,128)}), f32[8,4,64,128]{3,2,1,0:T(8,128)}, u32[]{:S(2)}, u32[]{:S(2)}) async-start(f32[8,4,64,128]{3,2,1,0:T(8,128)} %bitcast.137), calls=%async_computation.4 | async-start | bytes 2097152 | tf_op jit(solution)/shard_map/all_to_all | solution.py:15
  32.1 9.9 %all-to-all-done.4 = f32[8,4,64,128]{3,2,1,0:T(8,128)} async-done(((f32[8,4,64,128]{3,2,1,0:T(8,128)}), f32[8,4,64,128]{3,2,1,0:T(8,128)}, u32[]{:S(2)}, u32[]{:S(2)}) %all-to-all-start.4) | async-done | bytes 1048608 | tf_op jit(solution)/shard_map/all_to_all | solution.py:15
  42.1 4.9 all-to-all-start.1
  49.0 11.1 %all-to-all-done.1 = f32[8,4,64,128]{3,2,1,0:T(8,128)S(1)} async-done(((f32[8,4,64,128]{3,2,1,0:T(8,128)}), f32[8,4,64,128]{3,2,1,0:T(8,128)S(1)}, u32[]{:S(2)}, u32[]{:S(2)}) %all-to-all-start.1) | async-done | bytes 1048608 | tf_op jit(solution)/shard_map/all_to_all | solution.py:15
  60.1 11.2 %all-to-all-start.5 = ((bf16[4,64,128]{2,0,1:T(4,128)(2,1)}), bf16[4,64,128]{2,0,1:T(4,128)(2,1)S(1)}, u32[]{:S(2)}, u32[]{:S(2)}) async-start(bf16[4,64,128]{2,0,1:T(4,128)(2,1)} %copy.87), calls=%async_computation.5 | async-start | bytes 131072 | tf_op jit(solution)/shard_map/all_to_all | solution.py:71
  72.0 9.2 %all-to-all-done.5 = bf16[4,64,128]{2,0,1:T(4,128)(2,1)S(1)} async-done(((bf16[4,64,128]{2,0,1:T(4,128)(2,1)}), bf16[4,64,128]{2,0,1:T(4,128)(2,1)S(1)}, u32[]{:S(2)}, u32[]{:S(2)}) %all-to-all-start.5) | async-done | bytes 65568 | tf_op jit(solution)/shard_map/all_to_all | solution.py:71
  85.2 9.9 %all-to-all-done.2 = bf16[4,64,128]{2,0,1:T(4,128)(2,1)S(1)} async-done(((bf16[4,64,128]{2,0,1:T(4,128)(2,1)}), bf16[4,64,128]{2,0,1:T(4,128)(2,1)S(1)}, u32[]{:S(2)}, u32[]{:S(2)}) %all-to-all-start.2) | async-done | bytes 65568 | tf_op jit(solution)/shard_map/all_to_all | solution.py:71
  95.9 4.9 all-to-all-start.6
  100.9 8.5 %all-to-all-done.6 = bf16[8,128,2,128]{3,1,2,0:T(8,128)(2,1)S(1)} async-done(((bf16[8,128,2,128]{3,1,2,0:T(8,128)(2,1)}), bf16[8,128,2,128]{3,1,2,0:T(8,128)(2,1)S(1)}, u32[]{:S(2)}, u32[]{:S(2)}) %all-to-all-start.6) | async-done | bytes 524320 | tf_op jit(solution)/shard_map/all_to_all | solution.py:21
  110.3 5.5 %all-to-all-start.3 = ((bf16[8,128,2,128]{3,1,2,0:T(8,128)(2,1)}), bf16[8,128,2,128]{3,1,2,0:T(8,128)(2,1)}, u32[]{:S(2)}, u32[]{:S(2)}) async-start(bf16[8,128,2,128]{3,1,2,0:T(8,128)(2,1)} %broadcast_in_dim.22), calls=%async_computation.3 | async-start | bytes 1048576 | tf_op jit(solution)/shard_map/all_to_all | solution.py:21
  116.2 7.5 %all-to-all-done.3 = bf16[8,128,2,128]{3,1,2,0:T(8,128)(2,1)} async-done(((bf16[8,128,2,128]{3,1,2,0:T(8,128)(2,1)}), bf16[8,128,2,128]{3,1,2,0:T(8,128)(2,1)}, u32[]{:S(2)}, u32[]{:S(2)}) %all-to-all-start.3) | async-done | bytes 524320 | tf_op jit(solution)/shard_map/all_to_all | solution.py:21
  128.3 5.5 %all-to-all-start.7 = ((f32[8,128,2,128]{3,1,2,0:T(8,128)}), f32[8,128,2,128]{3,1,2,0:T(8,128)}, u32[]{:S(2)}, u32[]{:S(2)}) async-start(f32[8,128,2,128]{3,1,2,0:T(8,128)} %bitcast.142), calls=%async_computation.7 | async-start | bytes 2097152 | tf_op jit(solution)/shard_map/all_to_all | solution.py:15
  137.1 10.2 %all-to-all-done.7 = f32[8,128,2,128]{3,1,2,0:T(8,128)} async-done(((f32[8,128,2,128]{3,1,2,0:T(8,128)}), f32[8,128,2,128]{3,1,2,0:T(8,128)}, u32[]{:S(2)}, u32[]{:S(2)}) %all-to-all-start.7) | async-done | bytes 1048608 | tf_op jit(solution)/shard_map/all_to_all | solution.py:15
  147.3 5.6 %all-to-all-start.10 = ((f32[8,128,2,128]{3,1,2,0:T(8,128)}), f32[8,128,2,128]{3,1,2,0:T(8,128)}, u32[]{:S(2)}, u32[]{:S(2)}) async-start(f32[8,128,2,128]{3,1,2,0:T(8,128)} %bitcast.141), calls=%async_computation.10 | async-start | bytes 2097152 | tf_op jit(solution)/shard_map/all_to_all | solution.py:15
  156.3 9.6 %all-to-all-done.10 = f32[8,128,2,128]{3,1,2,0:T(8,128)} async-done(((f32[8,128,2,128]{3,1,2,0:T(8,128)}), f32[8,128,2,128]{3,1,2,0:T(8,128)}, u32[]{:S(2)}, u32[]{:S(2)}) %all-to-all-start.10) | async-done | bytes 1048608 | tf_op jit(solution)/shard_map/all_to_all | solution.py:15
  165.9 4.6 all-to-all-start.8
  173.9 6.5 %all-to-all-done.8 = bf16[128,2,128]{2,1,0:T(2,128)(2,1)} async-done(((bf16[128,2,128]{2,1,0:T(2,128)(2,1)}), bf16[128,2,128]{2,1,0:T(2,128)(2,1)}, u32[]{:S(2)}, u32[]{:S(2)}) %all-to-all-start.8) | async-done | bytes 65568 | tf_op jit(solution)/shard_map/all_to_all | solution.py:78
  180.4 4.6 all-to-all-start.11
  186.5 8.4 %all-to-all-done.11 = bf16[128,2,128]{2,1,0:T(2,128)(2,1)} async-done(((bf16[128,2,128]{2,1,0:T(2,128)(2,1)}), bf16[128,2,128]{2,1,0:T(2,128)(2,1)}, u32[]{:S(2)}, u32[]{:S(2)}) %all-to-all-start.11) | async-done | bytes 65568 | tf_op jit(solution)/shard_map/all_to_all | solution.py:78
  196.7 5.5 %all-to-all-start.9 = ((bf16[8,4,64,128]{3,2,1,0:T(8,128)(2,1)}), bf16[8,4,64,128]{3,2,1,0:T(8,128)(2,1)}, u32[]{:S(2)}, u32[]{:S(2)}) async-start(bf16[8,4,64,128]{3,2,1,0:T(8,128)(2,1)} %broadcast_in_dim.26), calls=%async_computation.9 | async-start | bytes 1048576 | tf_op jit(solution)/shard_map/all_to_all | solution.py:21
  211.8 5.5 %all-to-all-start.12 = ((bf16[8,4,64,128]{3,2,1,0:T(8,128)(2,1)}), bf16[8,4,64,128]{3,2,1,0:T(8,128)(2,1)}, u32[]{:S(2)}, u32[]{:S(2)}) async-start(bf16[8,4,64,128]{3,2,1,0:T(8,128)(2,1)} %broadcast_in_dim.28), calls=%async_computation.12 | async-start | bytes 1048576 | tf_op jit(solution)/shard_map/all_to_all | solution.py:21
  225.2 4.7 all-to-all-start.13
  242.2 245.3 %all-reduce.2.cloned.1.call-done = f32[1024,64]{0,1:T(8,128)} async-done(((f32[1024,64]{0,1:T(8,128)}), f32[1024,64]{0,1:T(8,128)}) %all-reduce.2.cloned.1.call-update) | async-done | bytes 262160 | tf_op jit(solution)/shard_map/psum | solution.py:144
  (72 shorter events, 67.4 us)
Async XLA Ops:
  7.2 108.6 %copy-start = (bf16[2,1024,512]{2,1,0:T(8,128)(2,1)S(1)}, bf16[2,1024,512]{2,1,0:T(8,128)(2,1)}, u32[]{:S(2)}) copy-start(bf16[2,1024,512]{2,1,0:T(8,128)(2,1)} %param.8) | copy-start | bytes 6291460
  20.9 199.2 %copy-start.2 = (f32[4,64]{1,0:T(4,128)}, f32[4,64]{1,0:T(4,128)S(1)}, u32[]{:S(2)}) copy-start(f32[4,64]{1,0:T(4,128)S(1)} %get-tuple-element.10) | copy-start | bytes 3076
  20.9 199.2 %copy-start.3 = (f32[4,64]{1,0:T(4,128)}, f32[4,64]{1,0:T(4,128)S(1)}, u32[]{:S(2)}) copy-start(f32[4,64]{1,0:T(4,128)S(1)} %get-tuple-element.11) | copy-start | bytes 3076
  23.4 18.7 %all-to-all-start.4 = ((f32[8,4,64,128]{3,2,1,0:T(8,128)}), f32[8,4,64,128]{3,2,1,0:T(8,128)}, u32[]{:S(2)}, u32[]{:S(2)}) async-start(f32[8,4,64,128]{3,2,1,0:T(8,128)} %bitcast.137), calls=%async_computation.4 | async-start | bytes 2097152 | tf_op jit(solution)/shard_map/all_to_all | solution.py:15
  29.7 12.4 %copy-start.4 = (f32[4,72]{1,0:T(4,128)}, f32[4,72]{1,0:T(4,128)S(1)}, u32[]{:S(2)}) copy-start(f32[4,72]{1,0:T(4,128)S(1)} %get-tuple-element.14) | copy-start | bytes 3460
  42.1 18.0 %all-to-all-start.1 = ((f32[8,4,64,128]{3,2,1,0:T(8,128)}), f32[8,4,64,128]{3,2,1,0:T(8,128)S(1)}, u32[]{:S(2)}, u32[]{:S(2)}) async-start(f32[8,4,64,128]{3,2,1,0:T(8,128)} %bitcast.140), calls=%async_computation.1 | async-start | bytes 2097152 | tf_op jit(solution)/shard_map/all_to_all | solution.py:15
  60.1 21.2 %all-to-all-start.5 = ((bf16[4,64,128]{2,0,1:T(4,128)(2,1)}), bf16[4,64,128]{2,0,1:T(4,128)(2,1)S(1)}, u32[]{:S(2)}, u32[]{:S(2)}) async-start(bf16[4,64,128]{2,0,1:T(4,128)(2,1)} %copy.87), calls=%async_computation.5 | async-start | bytes 131072 | tf_op jit(solution)/shard_map/all_to_all | solution.py:71
  81.2 13.8 %all-to-all-start.2 = ((bf16[4,64,128]{2,0,1:T(4,128)(2,1)}), bf16[4,64,128]{2,0,1:T(4,128)(2,1)S(1)}, u32[]{:S(2)}, u32[]{:S(2)}) async-start(bf16[4,64,128]{2,0,1:T(4,128)(2,1)} %copy.82), calls=%async_computation.2 | async-start | bytes 131072 | tf_op jit(solution)/shard_map/all_to_all | solution.py:71
  95.9 13.5 %all-to-all-start.6 = ((bf16[8,128,2,128]{3,1,2,0:T(8,128)(2,1)}), bf16[8,128,2,128]{3,1,2,0:T(8,128)(2,1)S(1)}, u32[]{:S(2)}, u32[]{:S(2)}) async-start(bf16[8,128,2,128]{3,1,2,0:T(8,128)(2,1)} %broadcast_in_dim.24), calls=%async_computation.6 | async-start | bytes 1048576 | tf_op jit(solution)/shard_map/all_to_all | solution.py:21
  110.3 13.4 %all-to-all-start.3 = ((bf16[8,128,2,128]{3,1,2,0:T(8,128)(2,1)}), bf16[8,128,2,128]{3,1,2,0:T(8,128)(2,1)}, u32[]{:S(2)}, u32[]{:S(2)}) async-start(bf16[8,128,2,128]{3,1,2,0:T(8,128)(2,1)} %broadcast_in_dim.22), calls=%async_computation.3 | async-start | bytes 1048576 | tf_op jit(solution)/shard_map/all_to_all | solution.py:21
  128.3 18.9 %all-to-all-start.7 = ((f32[8,128,2,128]{3,1,2,0:T(8,128)}), f32[8,128,2,128]{3,1,2,0:T(8,128)}, u32[]{:S(2)}, u32[]{:S(2)}) async-start(f32[8,128,2,128]{3,1,2,0:T(8,128)} %bitcast.142), calls=%async_computation.7 | async-start | bytes 2097152 | tf_op jit(solution)/shard_map/all_to_all | solution.py:15
  147.3 18.6 %all-to-all-start.10 = ((f32[8,128,2,128]{3,1,2,0:T(8,128)}), f32[8,128,2,128]{3,1,2,0:T(8,128)}, u32[]{:S(2)}, u32[]{:S(2)}) async-start(f32[8,128,2,128]{3,1,2,0:T(8,128)} %bitcast.141), calls=%async_computation.10 | async-start | bytes 2097152 | tf_op jit(solution)/shard_map/all_to_all | solution.py:15
  165.9 14.5 %all-to-all-start.8 = ((bf16[128,2,128]{2,1,0:T(2,128)(2,1)}), bf16[128,2,128]{2,1,0:T(2,128)(2,1)}, u32[]{:S(2)}, u32[]{:S(2)}) async-start(bf16[128,2,128]{2,1,0:T(2,128)(2,1)} %copy.92), calls=%async_computation.8 | async-start | bytes 131072 | tf_op jit(solution)/shard_map/all_to_all | solution.py:78
  180.4 14.5 %all-to-all-start.11 = ((bf16[128,2,128]{2,1,0:T(2,128)(2,1)}), bf16[128,2,128]{2,1,0:T(2,128)(2,1)}, u32[]{:S(2)}, u32[]{:S(2)}) async-start(bf16[128,2,128]{2,1,0:T(2,128)(2,1)} %copy.97), calls=%async_computation.11 | async-start | bytes 131072 | tf_op jit(solution)/shard_map/all_to_all | solution.py:78
  196.7 14.2 %all-to-all-start.9 = ((bf16[8,4,64,128]{3,2,1,0:T(8,128)(2,1)}), bf16[8,4,64,128]{3,2,1,0:T(8,128)(2,1)}, u32[]{:S(2)}, u32[]{:S(2)}) async-start(bf16[8,4,64,128]{3,2,1,0:T(8,128)(2,1)} %broadcast_in_dim.26), calls=%async_computation.9 | async-start | bytes 1048576 | tf_op jit(solution)/shard_map/all_to_all | solution.py:21
  211.8 13.4 %all-to-all-start.12 = ((bf16[8,4,64,128]{3,2,1,0:T(8,128)(2,1)}), bf16[8,4,64,128]{3,2,1,0:T(8,128)(2,1)}, u32[]{:S(2)}, u32[]{:S(2)}) async-start(bf16[8,4,64,128]{3,2,1,0:T(8,128)(2,1)} %broadcast_in_dim.28), calls=%async_computation.12 | async-start | bytes 1048576 | tf_op jit(solution)/shard_map/all_to_all | solution.py:21
  221.6 18.1 %copy-start.1 = (bf16[1024,64]{0,1:T(8,128)(2,1)S(1)}, bf16[1024,64]{0,1:T(8,128)(2,1)}, u32[]{:S(2)}) copy-start(bf16[1024,64]{0,1:T(8,128)(2,1)} %param.7) | copy-start | bytes 393220
  225.2 9.4 %all-to-all-start.13 = ((f32[8,1,256]{2,1,0:T(1,128)}), f32[8,1,256]{2,1,0:T(1,128)S(1)}, u32[]{:S(2)}, u32[]{:S(2)}) async-start(f32[8,1,256]{2,1,0:T(1,128)} %reshape.65), calls=%async_computation.13 | async-start | bytes 16384 | tf_op jit(solution)/shard_map/all_to_all | solution.py:21
  229.9 257.6 %all-reduce.2.cloned.1.call-start = ((), (), s32[]{:S(2)}) async-start(), calls=%async_computation.14 | async-start | bytes 524288 | tf_op jit(solution)/shard_map/psum | solution.py:144
Sparse Core Ops, SparseCore 0:
  239.8 247.6 all-reduce.1
where the time goes:
time: 498 us; the launch traced here: 496 us
  waiting for transfers between devices  345 us (69%)
  starting transfers between devices  71.8 us (14%)
  matrix products  26.7 us (5%)
  local copies, waits for them, and re-layouts  19.7 us (4%)
  between operations  14.3 us (3%)
  blocking collectives  10.4 us (2%)
  other arithmetic  8.52 us (2%)
    psum x1, waiting for transfers between devices, on_device(): grad_router = lax.psum(local_router, ('dp', 'tensor'))  245 us
    all_to_all x4, waiting for transfers between devices, summed_on_arrival(): lax.all_to_all(blocks, axis, split_axis=0, concat_axis=0, tiled=True)  40.8 us
    all_to_all x5, starting transfers between devices, sent_to_all(): lax.all_to_all(jnp.broadcast_to(x[None], (length, *x.shape)), axis, 0, 0,...  26 us
    all_to_all x5, waiting for transfers between devices, sent_to_all(): lax.all_to_all(jnp.broadcast_to(x[None], (length, *x.shape)), axis, 0, 0,...  24.6 us
    all_to_all x4, starting transfers between devices, summed_on_arrival(): lax.all_to_all(blocks, axis, split_axis=0, concat_axis=0, tiled=True)  21.6 us
    all_to_all x2, waiting for transfers between devices, to_experts(): lax.all_to_all(shared_part, 'dp', split_axis=1, concat_axis=0, tiled=True)  19.1 us
    all_to_all x2, starting transfers between devices, to_experts(): lax.all_to_all(shared_part, 'dp', split_axis=1, concat_axis=0, tiled=True)  15.1 us
    all_to_all x2, waiting for transfers between devices, to_images(): lax.all_to_all(shared_part, 'dp', split_axis=0, concat_axis=1, tiled=True)  14.8 us
  transfers between devices with their start and end apart: 14, of which 14 were waited for; matrix products, arithmetic and copies ran while one was open for 7% of the time, Pallas kernels for 0%

commit v1 on v0

--- a/solution.py
+++ b/solution.py
@@ -2,6 +2,14 @@
 import jax.numpy as jnp
 from jax import lax
 from jax.sharding import PartitionSpec as P
+
+
+def _form_heads(message):
+    kept_arr = jnp.concatenate(
+        lax.all_to_all(jnp.stack(jnp.split(message, lax.axis_size("dp"), axis=0)), "dp", 0, 0),
+        axis=1,
+    )
+    return kept_arr
 
 
 def split_up(x, dim, length):
@@ -75,7 +83,7 @@
 
 def to_images(partial_rows):
     shared_part = summed_on_arrival(partial_rows, "tensor", 2).astype(jnp.bfloat16)
-    arrived = lax.all_to_all(shared_part, "dp", split_axis=0, concat_axis=1, tiled=True)
+    arrived = _form_heads(shared_part)
     result = gathered_copies(arrived, "tensor", 2)
     return result
 

time: 498 us -> 532 us (1.068)
  local copies, waits for them, and re-layouts: 19.7 us -> 62.6 us
  waiting for transfers between devices: 345 us -> 329 us
  starting transfers between devices: 71.8 us -> 77.3 us
    unnamed x15 -> x79, local copies, waits for them, and re-layouts: 3.32 us -> 46.6 us
    all_to_all x4, waiting for transfers between devices: 40.8 us -> 31.2 us  [summed_on_arrival(): lax.all_to_all(blocks, axis, split_axis=0, concat_axis=0, tiled=True)]
    all_to_all x2, waiting for transfers between devices: 14.8 us -> 8.41 us  [_form_heads(): lax.all_to_all(jnp.stack(jnp.split(message, lax.axis_size('dp'), axis=0))...]
  transfers between devices with their start and end apart: 14 -> 14, of which waited for: 14 -> 12; matrix products, arithmetic and copies ran while one was open for 7% -> 14% of each run, Pallas kernels for 0% -> 0%
where the time goes in v1:
time: 532 us; the launch traced here: 529 us
  waiting for transfers between devices  329 us (62%)
  starting transfers between devices  77.3 us (15%)
  local copies, waits for them, and re-layouts  62.6 us (12%)
  matrix products  26.6 us (5%)
  between operations  14.3 us (3%)
  blocking collectives  10.4 us (2%)
  other arithmetic  8.52 us (2%)
    psum x1, waiting for transfers between devices, on_device(): grad_router = lax.psum(local_router, ('dp', 'tensor'))  246 us
    unnamed x79, local copies, waits for them, and re-layouts  46.6 us
    all_to_all x4, waiting for transfers between devices, summed_on_arrival(): lax.all_to_all(blocks, axis, split_axis=0, concat_axis=0, tiled=True)  31.2 us
    all_to_all x5, starting transfers between devices, sent_to_all(): lax.all_to_all(jnp.broadcast_to(x[None], (length, *x.shape)), axis, 0, 0,...  26.3 us
    all_to_all x5, waiting for transfers between devices, sent_to_all(): lax.all_to_all(jnp.broadcast_to(x[None], (length, *x.shape)), axis, 0, 0,...  24.5 us
    all_to_all x4, starting transfers between devices, summed_on_arrival(): lax.all_to_all(blocks, axis, split_axis=0, concat_axis=0, tiled=True)  21.6 us
    all_to_all x2, waiting for transfers between devices, to_experts(): lax.all_to_all(shared_part, 'dp', split_axis=1, concat_axis=0, tiled=True)  19.1 us
    all_to_all x2, starting transfers between devices, to_experts(): lax.all_to_all(shared_part, 'dp', split_axis=1, concat_axis=0, tiled=True)  15.1 us
  transfers between devices with their start and end apart: 14, of which 12 were waited for; matrix products, arithmetic and copies ran while one was open for 14% of the time, Pallas kernels for 0%

profile of v1, /device:TPU:2, one launch (start us, length us, event | category | flops | bytes accessed | tf_op | source)
XLA Modules:
  0.0 528.8 jit_solution(11367866629655111393)
XLA Ops:
  9.2 10.4 %all_to_all.90 = f32[8,1,512]{2,1,0:T(1,128)S(1)} all-to-all(f32[8,1,512]{2,1,0:T(1,128)S(1)} %reshape.69), channel_id=1, replica_groups=mesh['dp'=32,'tensor'=8] {'tensor'}, dimensions={0} | all-to-all | bytes 32768 | tf_op jit(solution)/shard_map/all_to_all | solution.py:29
  23.4 5.6 %all-to-all-start.4 = ((f32[8,4,64,128]{3,2,1,0:T(8,128)}), f32[8,4,64,128]{3,2,1,0:T(8,128)}, u32[]{:S(2)}, u32[]{:S(2)}) async-start(f32[8,4,64,128]{3,2,1,0:T(8,128)} %bitcast.389), calls=%async_computation.4 | async-start | bytes 2097152 | tf_op jit(solution)/shard_map/all_to_all | solution.py:23
  32.1 9.9 %all-to-all-done.4 = f32[8,4,64,128]{3,2,1,0:T(8,128)} async-done(((f32[8,4,64,128]{3,2,1,0:T(8,128)}), f32[8,4,64,128]{3,2,1,0:T(8,128)}, u32[]{:S(2)}, u32[]{:S(2)}) %all-to-all-start.4) | async-done | bytes 1048608 | tf_op jit(solution)/shard_map/all_to_all | solution.py:23
  42.1 4.9 all-to-all-start.1
  49.0 11.1 %all-to-all-done.1 = f32[8,4,64,128]{3,2,1,0:T(8,128)S(1)} async-done(((f32[8,4,64,128]{3,2,1,0:T(8,128)}), f32[8,4,64,128]{3,2,1,0:T(8,128)S(1)}, u32[]{:S(2)}, u32[]{:S(2)}) %all-to-all-start.1) | async-done | bytes 1048608 | tf_op jit(solution)/shard_map/all_to_all | solution.py:23
  60.1 11.2 %all-to-all-start.5 = ((bf16[4,64,128]{2,0,1:T(4,128)(2,1)}), bf16[4,64,128]{2,0,1:T(4,128)(2,1)S(1)}, u32[]{:S(2)}, u32[]{:S(2)}) async-start(bf16[4,64,128]{2,0,1:T(4,128)(2,1)} %copy.291), calls=%async_computation.5 | async-start | bytes 131072 | tf_op jit(solution)/shard_map/all_to_all | solution.py:79
  72.0 9.2 %all-to-all-done.5 = bf16[4,64,128]{2,0,1:T(4,128)(2,1)S(1)} async-done(((bf16[4,64,128]{2,0,1:T(4,128)(2,1)}), bf16[4,64,128]{2,0,1:T(4,128)(2,1)S(1)}, u32[]{:S(2)}, u32[]{:S(2)}) %all-to-all-start.5) | async-done | bytes 65568 | tf_op jit(solution)/shard_map/all_to_all | solution.py:79
  81.2 3.9 all-to-all-start.2
  85.2 9.9 %all-to-all-done.2 = bf16[4,64,128]{2,0,1:T(4,128)(2,1)S(1)} async-done(((bf16[4,64,128]{2,0,1:T(4,128)(2,1)}), bf16[4,64,128]{2,0,1:T(4,128)(2,1)S(1)}, u32[]{:S(2)}, u32[]{:S(2)}) %all-to-all-start.2) | async-done | bytes 65568 | tf_op jit(solution)/shard_map/all_to_all | solution.py:79
  95.9 4.9 all-to-all-start.6
  100.9 8.5 %all-to-all-done.6 = bf16[8,128,2,128]{3,1,2,0:T(8,128)(2,1)S(1)} async-done(((bf16[8,128,2,128]{3,1,2,0:T(8,128)(2,1)}), bf16[8,128,2,128]{3,1,2,0:T(8,128)(2,1)S(1)}, u32[]{:S(2)}, u32[]{:S(2)}) %all-to-all-start.6) | async-done | bytes 524320 | tf_op jit(solution)/shard_map/all_to_all | solution.py:29
  110.3 5.5 %all-to-all-start.3 = ((bf16[8,128,2,128]{3,1,2,0:T(8,128)(2,1)}), bf16[8,128,2,128]{3,1,2,0:T(8,128)(2,1)}, u32[]{:S(2)}, u32[]{:S(2)}) async-start(bf16[8,128,2,128]{3,1,2,0:T(8,128)(2,1)} %broadcast_in_dim.22), calls=%async_computation.3 | async-start | bytes 1048576 | tf_op jit(solution)/shard_map/all_to_all | solution.py:29
  116.2 7.5 %all-to-all-done.3 = bf16[8,128,2,128]{3,1,2,0:T(8,128)(2,1)} async-done(((bf16[8,128,2,128]{3,1,2,0:T(8,128)(2,1)}), bf16[8,128,2,128]{3,1,2,0:T(8,128)(2,1)}, u32[]{:S(2)}, u32[]{:S(2)}) %all-to-all-start.3) | async-done | bytes 524320 | tf_op jit(solution)/shard_map/all_to_all | solution.py:29
  128.3 5.5 %all-to-all-start.7 = ((f32[8,128,2,128]{3,1,2,0:T(8,128)}), f32[8,128,2,128]{3,1,2,0:T(8,128)}, u32[]{:S(2)}, u32[]{:S(2)}) async-start(f32[8,128,2,128]{3,1,2,0:T(8,128)} %bitcast.394), calls=%async_computation.7 | async-start | bytes 2097152 | tf_op jit(solution)/shard_map/all_to_all | solution.py:23
  137.1 10.2 %all-to-all-done.7 = f32[8,128,2,128]{3,1,2,0:T(8,128)} async-done(((f32[8,128,2,128]{3,1,2,0:T(8,128)}), f32[8,128,2,128]{3,1,2,0:T(8,128)}, u32[]{:S(2)}, u32[]{:S(2)}) %all-to-all-start.7) | async-done | bytes 1048608 | tf_op jit(solution)/shard_map/all_to_all | solution.py:23
  147.3 5.6 %all-to-all-start.10 = ((f32[8,128,2,128]{3,1,2,0:T(8,128)}), f32[8,128,2,128]{3,1,2,0:T(8,128)}, u32[]{:S(2)}, u32[]{:S(2)}) async-start(f32[8,128,2,128]{3,1,2,0:T(8,128)} %bitcast.392), calls=%async_computation.10 | async-start | bytes 2097152 | tf_op jit(solution)/shard_map/all_to_all | solution.py:23
  177.7 4.6 all-to-all-start.8
  207.3 9.8 %all-to-all-start.11 = ((bf16[32,4,2,128]{3,2,1,0:T(2,128)(2,1)}), bf16[32,4,2,128]{3,2,1,0:T(2,128)(2,1)}, u32[]{:S(2)}, u32[]{:S(2)}) async-start(bf16[32,4,2,128]{3,2,1,0:T(2,128)(2,1)} %copy.302), calls=%async_computation.11 | async-start | bytes 131072 | tf_op jit(solution)/shard_map/all_to_all | solution.py:9
  218.7 8.4 %all-to-all-done.11 = bf16[32,4,2,128]{3,2,1,0:T(2,128)(2,1)} async-done(((bf16[32,4,2,128]{3,2,1,0:T(2,128)(2,1)}), bf16[32,4,2,128]{3,2,1,0:T(2,128)(2,1)}, u32[]{:S(2)}, u32[]{:S(2)}) %all-to-all-start.11) | async-done | bytes 65568 | tf_op jit(solution)/shard_map/all_to_all | solution.py:9
  228.8 5.7 %all-to-all-start.9 = ((bf16[8,4,64,128]{3,2,1,0:T(8,128)(2,1)}), bf16[8,4,64,128]{3,2,1,0:T(8,128)(2,1)}, u32[]{:S(2)}, u32[]{:S(2)}) async-start(bf16[8,4,64,128]{3,2,1,0:T(8,128)(2,1)} %broadcast_in_dim.26), calls=%async_computation.9 | async-start | bytes 1048576 | tf_op jit(solution)/shard_map/all_to_all | solution.py:29
  243.9 5.5 %all-to-all-start.12 = ((bf16[8,4,64,128]{3,2,1,0:T(8,128)(2,1)}), bf16[8,4,64,128]{3,2,1,0:T(8,128)(2,1)}, u32[]{:S(2)}, u32[]{:S(2)}) async-start(bf16[8,4,64,128]{3,2,1,0:T(8,128)(2,1)} %broadcast_in_dim.55), calls=%async_computation.12 | async-start | bytes 1048576 | tf_op jit(solution)/shard_map/all_to_all | solution.py:29
  253.6 3.7 all-to-all-done.12
  257.3 4.7 all-to-all-start.13
  274.3 245.9 %all-reduce.2.cloned.1.call-done = f32[1024,64]{0,1:T(8,128)} async-done(((f32[1024,64]{0,1:T(8,128)}), f32[1024,64]{0,1:T(8,128)}) %all-reduce.2.cloned.1.call-update) | async-done | bytes 262160 | tf_op jit(solution)/shard_map/psum | solution.py:152
  (136 shorter events, 102.5 us)
Async XLA Ops:
  7.2 108.6 %copy-start = (bf16[2,1024,512]{2,1,0:T(8,128)(2,1)S(1)}, bf16[2,1024,512]{2,1,0:T(8,128)(2,1)}, u32[]{:S(2)}) copy-start(bf16[2,1024,512]{2,1,0:T(8,128)(2,1)} %param.8) | copy-start | bytes 6291460
  20.9 231.2 %copy-start.3 = (f32[4,64]{1,0:T(4,128)}, f32[4,64]{1,0:T(4,128)S(1)}, u32[]{:S(2)}) copy-start(f32[4,64]{1,0:T(4,128)S(1)} %get-tuple-element.10) | copy-start | bytes 3076
  20.9 231.2 %copy-start.4 = (f32[4,64]{1,0:T(4,128)}, f32[4,64]{1,0:T(4,128)S(1)}, u32[]{:S(2)}) copy-start(f32[4,64]{1,0:T(4,128)S(1)} %get-tuple-element.11) | copy-start | bytes 3076
  23.4 18.7 %all-to-all-start.4 = ((f32[8,4,64,128]{3,2,1,0:T(8,128)}), f32[8,4,64,128]{3,2,1,0:T(8,128)}, u32[]{:S(2)}, u32[]{:S(2)}) async-start(f32[8,4,64,128]{3,2,1,0:T(8,128)} %bitcast.389), calls=%async_computation.4 | async-start | bytes 2097152 | tf_op jit(solution)/shard_map/all_to_all | solution.py:23
  29.7 12.4 %copy-start.5 = (f32[4,72]{1,0:T(4,128)}, f32[4,72]{1,0:T(4,128)S(1)}, u32[]{:S(2)}) copy-start(f32[4,72]{1,0:T(4,128)S(1)} %get-tuple-element.14) | copy-start | bytes 3460
  42.1 18.0 %all-to-all-start.1 = ((f32[8,4,64,128]{3,2,1,0:T(8,128)}), f32[8,4,64,128]{3,2,1,0:T(8,128)S(1)}, u32[]{:S(2)}, u32[]{:S(2)}) async-start(f32[8,4,64,128]{3,2,1,0:T(8,128)} %bitcast.393), calls=%async_computation.1 | async-start | bytes 2097152 | tf_op jit(solution)/shard_map/all_to_all | solution.py:23
  60.1 21.2 %all-to-all-start.5 = ((bf16[4,64,128]{2,0,1:T(4,128)(2,1)}), bf16[4,64,128]{2,0,1:T(4,128)(2,1)S(1)}, u32[]{:S(2)}, u32[]{:S(2)}) async-start(bf16[4,64,128]{2,0,1:T(4,128)(2,1)} %copy.291), calls=%async_computation.5 | async-start | bytes 131072 | tf_op jit(solution)/shard_map/all_to_all | solution.py:79
  81.2 13.8 %all-to-all-start.2 = ((bf16[4,64,128]{2,0,1:T(4,128)(2,1)}), bf16[4,64,128]{2,0,1:T(4,128)(2,1)S(1)}, u32[]{:S(2)}, u32[]{:S(2)}) async-start(bf16[4,64,128]{2,0,1:T(4,128)(2,1)} %copy.286), calls=%async_computation.2 | async-start | bytes 131072 | tf_op jit(solution)/shard_map/all_to_all | solution.py:79
  95.9 13.5 %all-to-all-start.6 = ((bf16[8,128,2,128]{3,1,2,0:T(8,128)(2,1)}), bf16[8,128,2,128]{3,1,2,0:T(8,128)(2,1)S(1)}, u32[]{:S(2)}, u32[]{:S(2)}) async-start(bf16[8,128,2,128]{3,1,2,0:T(8,128)(2,1)} %broadcast_in_dim.24), calls=%async_computation.6 | async-start | bytes 1048576 | tf_op jit(solution)/shard_map/all_to_all | solution.py:29
  110.3 13.4 %all-to-all-start.3 = ((bf16[8,128,2,128]{3,1,2,0:T(8,128)(2,1)}), bf16[8,128,2,128]{3,1,2,0:T(8,128)(2,1)}, u32[]{:S(2)}, u32[]{:S(2)}) async-start(bf16[8,128,2,128]{3,1,2,0:T(8,128)(2,1)} %broadcast_in_dim.22), calls=%async_computation.3 | async-start | bytes 1048576 | tf_op jit(solution)/shard_map/all_to_all | solution.py:29
  128.3 18.9 %all-to-all-start.7 = ((f32[8,128,2,128]{3,1,2,0:T(8,128)}), f32[8,128,2,128]{3,1,2,0:T(8,128)}, u32[]{:S(2)}, u32[]{:S(2)}) async-start(f32[8,128,2,128]{3,1,2,0:T(8,128)} %bitcast.394), calls=%async_computation.7 | async-start | bytes 2097152 | tf_op jit(solution)/shard_map/all_to_all | solution.py:23
  147.3 30.5 %all-to-all-start.10 = ((f32[8,128,2,128]{3,1,2,0:T(8,128)}), f32[8,128,2,128]{3,1,2,0:T(8,128)}, u32[]{:S(2)}, u32[]{:S(2)}) async-start(f32[8,128,2,128]{3,1,2,0:T(8,128)} %bitcast.392), calls=%async_computation.10 | async-start | bytes 2097152 | tf_op jit(solution)/shard_map/all_to_all | solution.py:23
  177.7 29.6 %all-to-all-start.8 = ((bf16[32,4,2,128]{3,2,1,0:T(2,128)(2,1)}), bf16[32,4,2,128]{3,2,1,0:T(2,128)(2,1)}, u32[]{:S(2)}, u32[]{:S(2)}) async-start(bf16[32,4,2,128]{3,2,1,0:T(2,128)(2,1)} %copy.297), calls=%async_computation.8 | async-start | bytes 131072 | tf_op jit(solution)/shard_map/all_to_all | solution.py:9
  207.3 19.8 %all-to-all-start.11 = ((bf16[32,4,2,128]{3,2,1,0:T(2,128)(2,1)}), bf16[32,4,2,128]{3,2,1,0:T(2,128)(2,1)}, u32[]{:S(2)}, u32[]{:S(2)}) async-start(bf16[32,4,2,128]{3,2,1,0:T(2,128)(2,1)} %copy.302), calls=%async_computation.11 | async-start | bytes 131072 | tf_op jit(solution)/shard_map/all_to_all | solution.py:9
  228.8 14.1 %all-to-all-start.9 = ((bf16[8,4,64,128]{3,2,1,0:T(8,128)(2,1)}), bf16[8,4,64,128]{3,2,1,0:T(8,128)(2,1)}, u32[]{:S(2)}, u32[]{:S(2)}) async-start(bf16[8,4,64,128]{3,2,1,0:T(8,128)(2,1)} %broadcast_in_dim.26), calls=%async_computation.9 | async-start | bytes 1048576 | tf_op jit(solution)/shard_map/all_to_all | solution.py:29
  236.6 12.7 %copy-start.1 = (bf16[4,72,1024]{2,1,0:T(8,128)(2,1)S(1)}, bf16[4,72,1024]{2,1,0:T(8,128)(2,1)}, u32[]{:S(2)}) copy-start(bf16[4,72,1024]{2,1,0:T(8,128)(2,1)} %param.5) | copy-start | bytes 1769476
  243.9 13.4 %all-to-all-start.12 = ((bf16[8,4,64,128]{3,2,1,0:T(8,128)(2,1)}), bf16[8,4,64,128]{3,2,1,0:T(8,128)(2,1)}, u32[]{:S(2)}, u32[]{:S(2)}) async-start(bf16[8,4,64,128]{3,2,1,0:T(8,128)(2,1)} %broadcast_in_dim.55), calls=%async_computation.12 | async-start | bytes 1048576 | tf_op jit(solution)/shard_map/all_to_all | solution.py:29
  253.6 18.3 %copy-start.2 = (bf16[1024,64]{0,1:T(8,128)(2,1)S(1)}, bf16[1024,64]{0,1:T(8,128)(2,1)}, u32[]{:S(2)}) copy-start(bf16[1024,64]{0,1:T(8,128)(2,1)} %param.7) | copy-start | bytes 393220
  257.3 9.4 %all-to-all-start.13 = ((f32[8,1,256]{2,1,0:T(1,128)}), f32[8,1,256]{2,1,0:T(1,128)S(1)}, u32[]{:S(2)}, u32[]{:S(2)}) async-start(f32[8,1,256]{2,1,0:T(1,128)} %reshape.71), calls=%async_computation.13 | async-start | bytes 16384 | tf_op jit(solution)/shard_map/all_to_all | solution.py:29
  262.0 258.2 %all-reduce.2.cloned.1.call-start = ((), (), s32[]{:S(2)}) async-start(), calls=%async_computation.14 | async-start | bytes 524288 | tf_op jit(solution)/shard_map/psum | solution.py:152
Sparse Core Ops, SparseCore 0:
  272.0 248.2 all-reduce.1
